TPU v7x, 32 devices: a whole 2x2x4 slice. The times are simulated.
32 devices in a mesh: row: 4 (over y, x), col: 2 (over core), depth: 4 (over z).
Axes of the slice: x: 2, y: 2, z: 4, core: 2. Of those that a mesh axis runs over, the one named last changes fastest.
Arguments:
- a_cols: float32 [4096, 1024], P(('row', 'col')), may hold values from -16 to 24, as said below
- past_panels: float32 [4096, 2048], P(('row', 'col'), 'depth'), may hold values from -1 to 1
Outputs:
- factor: float32 [4096, 1024], P(('row', 'col'))
Inputs may be any that keep to these rules, and one draw needn't show every extreme that they name: a_cols minus past_panels times the transpose of the top 1024 rows of past_panels is the first 1024 columns of a symmetric positive definite matrix whose top block has eigenvalues between 2 and 12.
All inputs are finite; a program needn't handle non-finite values.
Results may differ from a plain program's by a relative error of at most 0.0001.
Values sent between devices are 32-bit elements.
A program may use at most 64 MiB of HBM per device.

v0:
```python
import jax
import jax.numpy as jnp
from jax import lax
from jax.sharding import PartitionSpec as P

NB = 512
STEPS = 2


def spread(array, axis, root):
    mine = lax.axis_index(axis) == root
    return lax.psum(jnp.where(mine, array, jnp.zeros_like(array)), axis)


def outer_rows(left, right):
    return lax.dot_general(
        left,
        right,
        (((1,), (1,)), ((), ())),
        precision=lax.Precision.HIGHEST,
        preferred_element_type=jnp.float32,
    )


def body(a_cols, past_panels):
    local_rows = a_cols.shape[0]
    position = lax.axis_index(("row", "col"))
    row_ids = position * local_rows + lax.broadcasted_iota(jnp.int32, (local_rows, NB), 0)
    col_ids = lax.broadcasted_iota(jnp.int32, (local_rows, NB), 1)
    result = jnp.zeros(a_cols.shape, jnp.float32)
    for section in range(STEPS):
        start = section * NB
        root = start // local_rows
        above = spread(past_panels, ("row", "col"), root)
        partial_value = outer_rows(past_panels, above)
        if section > 0:
            layer = lax.axis_index("depth")
            owned_ids = [layer + 0]
            owned_cols = [
                lax.dynamic_slice_in_dim(result, jnp.minimum(index, section - 1) * NB, NB, 1)
                for index in owned_ids
            ]
            sent_rows = jnp.stack([block for block in owned_cols])
            got_rows = spread(sent_rows, ("row", "col"), root)
            weight = (owned_ids[0] < section).astype(jnp.float32)
            partial_value = partial_value + weight * outer_rows(owned_cols[0], got_rows[0])
        summed = lax.psum(partial_value, "depth")
        update = a_cols[:, start : start + NB] - summed
        block = spread(update, ("row", "col"), root)
        diag_factor = jnp.linalg.cholesky(block)
        solved = jax.scipy.linalg.solve_triangular(diag_factor, update.T, lower=True).T
        new_panel = jnp.where(row_ids >= start + col_ids, solved, jnp.float32(0.0))
        result = result.at[:, start : start + NB].set(new_panel)
    return result


def solution(mesh):
    in_specs = (P(("row", "col"), None), P(("row", "col"), "depth"))
    out_specs = P(("row", "col"), None)
    return jax.shard_map(body, mesh=mesh, in_specs=in_specs, out_specs=out_specs, check_vma=False)
```

profile of v0, /device:TPU:27, one launch (start us, length us, event | category | flops | bytes accessed | tf_op | source)
XLA Modules:
  0.0 668.7 jit_solution(3477876616623234303)
XLA Ops:
  6.5 1.6 copy.4
  8.1 1.7 broadcast_select_fusion.3
  9.8 56.3 %all-reduce.10.cloned.1.call-done = f32[512,512]{0,1:T(8,128)} async-done(((f32[512,512]{0,1:T(8,128)}), f32[512,512]{0,1:T(8,128)}) %all-reduce.10.cloned.1.call-update) | async-done | bytes 1048592 | tf_op jit(solution)/shard_map/psum | solution.py:12
  66.2 5.7 convolution_bitcast_fusion.1
  72.0 2.7 fusion.69
  75.0 48.7 %all-reduce.12.cloned.1.call-done = f32[512,512]{0,1:T(8,128)} async-done(((f32[512,512]{0,1:T(8,128)}), f32[512,512]{0,1:T(8,128)}) %all-reduce.12.cloned.1.call-update) | async-done | bytes 1048592 | tf_op jit(solution)/shard_map/psum | solution.py:47
  123.7 2.8 broadcast_select_fusion.2
  127.5 54.9 %all-reduce.14.cloned.1.call-done = f32[512,512]{0,1:T(8,128)} async-done(((f32[512,512]{0,1:T(8,128)}), f32[512,512]{0,1:T(8,128)}) %all-reduce.14.cloned.1.call-update) | async-done | bytes 1048592 | tf_op jit(solution)/shard_map/psum | solution.py:12
  182.4 1.6 copy.5
  185.3 11.7 %cholesky.286 = f32[128,128]{1,0:T(8,128)S(1)} custom-call(f32[128,128]{1,0:T(8,128)S(1)} %cholesky.426), custom_call_target="Cholesky" | custom-call | tf_op jit(solution)/shard_map/jit(cholesky)/cholesky | solution.py:50
  197.0 9.8 %custom-call.27 = f32[1,128,128]{1,2,0:T(8,128)S(1)} custom-call(f32[1,128,128]{2,1,0:T(8,128)S(1)} %get-tuple-element.96), custom_call_target="InvertDiagBlocksLowerTriangular" | custom-call | tf_op jit(solution)/shard_map/jit(cholesky)/cholesky | solution.py:50
  209.5 11.7 %cholesky.305 = f32[128,128]{1,0:T(8,128)S(1)} custom-call(f32[128,128]{1,0:T(8,128)S(1)} %cholesky.430), custom_call_target="Cholesky" | custom-call | tf_op jit(solution)/shard_map/jit(cholesky)/cholesky | solution.py:50
  221.2 10.3 %custom-call.28 = f32[1,128,128]{1,2,0:T(8,128)S(1)} custom-call(f32[1,128,128]{2,1,0:T(8,128)S(1)} %get-tuple-element.93), custom_call_target="InvertDiagBlocksLowerTriangular" | custom-call | tf_op jit(solution)/shard_map/jit(cholesky)/cholesky | solution.py:50
  231.8 1.3 convolution_subtract_fusion.9
  233.1 11.7 %cholesky.326 = f32[128,128]{1,0:T(8,128)S(1)} custom-call(f32[128,128]{1,0:T(8,128)S(1)} %cholesky.435), custom_call_target="Cholesky" | custom-call | tf_op jit(solution)/shard_map/jit(cholesky)/cholesky | solution.py:50
  245.5 9.8 %custom-call.29 = f32[1,128,128]{1,2,0:T(8,128)S(1)} custom-call(f32[1,128,128]{2,1,0:T(8,128)S(1)} %get-tuple-element.90), custom_call_target="InvertDiagBlocksLowerTriangular" | custom-call | tf_op jit(solution)/shard_map/jit(cholesky)/cholesky | solution.py:50
  256.7 11.7 %cholesky.343 = f32[128,128]{1,0:T(8,128)S(1)} custom-call(f32[128,128]{1,0:T(8,128)S(1)} %convolution_subtract_fusion.11), custom_call_target="Cholesky" | custom-call | tf_op jit(solution)/shard_map/jit(cholesky)/cholesky | solution.py:50
  273.6 11.1 %while.6 = (s32[]{:T(128)}, f32[512,512]{1,0:T(8,128)}, s32[4,2]{0,1:T(2,128)S(1)}, f32[4,128,128]{2,1,0:T(8,128)S(1)}, s32[]{:T(128)}) while((s32[]{:T(128)}, f32[512,512]{1,0:T(8,128)}, s32[4,2]{0,1:T(2,128)S(1)}, f32[4,128,128]{2,1,0:T(8,128)S(1)}, s32[]{:T(128)}) %tuple.63), condition=%wide.while_cond.2, body=%wide.while_body.2.sunk | while | flops 2 | bytes 131181 | solution.py:51
  274.2 2.2 bitcast_dynamic-update-slice_fusion.4
  277.0 2.2 bitcast_dynamic-update-slice_fusion.4
  279.8 2.2 bitcast_dynamic-update-slice_fusion.4
  282.6 2.1 bitcast_dynamic-update-slice_fusion.4
  284.7 39.3 %custom-call.30 = f32[4,128,128]{1,2,0:T(8,128)S(1)} custom-call(f32[4,128,128]{2,1,0:T(8,128)S(1)} %get-tuple-element.45), custom_call_target="InvertDiagBlocksLowerTriangular" | custom-call | tf_op jit(solution)/shard_map/jit(_solve_triangular)/triangular_solve | solution.py:51
  326.1 1.3 convolution_subtract_fusion.2
  327.8 1.6 convolution_subtract_fusion.5
  331.8 61.5 %all-reduce.20.cloned.1.call-done = (f32[512,512]{0,1:T(8,128)}, f32[512,512]{0,1:T(8,128)}) async-done(((f32[512,512]{0,1:T(8,128)}, f32[512,512]{0,1:T(8,128)}), (f32[512,512]{0,1:T(8,128)}, f32[512,512]{0,1:T(8,128)})) %all-reduce.20.cloned.1.call-update) | async-done | bytes 2097168 | tf_op jit(solution)/shard_map/psum | solution.py:12
  393.3 4.8 convolution_bitcast_fusion
  398.1 2.9 fusion
  401.7 50.6 %all-reduce.16.cloned.1.call-done = f32[512,512]{0,1:T(8,128)} async-done(((f32[512,512]{0,1:T(8,128)}), f32[512,512]{0,1:T(8,128)}) %all-reduce.16.cloned.1.call-update) | async-done | bytes 1048592 | tf_op jit(solution)/shard_map/psum | solution.py:47
  452.3 2.8 broadcast_select_fusion
  455.1 55.8 %all-reduce.18.cloned.1.call-done = f32[512,512]{0,1:T(8,128)} async-done(((f32[512,512]{0,1:T(8,128)}), f32[512,512]{0,1:T(8,128)}) %all-reduce.18.cloned.1.call-update) | async-done | bytes 1048592 | tf_op jit(solution)/shard_map/psum | solution.py:12
  510.9 1.6 copy.9
  513.8 11.7 %cholesky.358 = f32[128,128]{1,0:T(8,128)S(1)} custom-call(f32[128,128]{1,0:T(8,128)S(1)} %cholesky.439), custom_call_target="Cholesky" | custom-call | tf_op jit(solution)/shard_map/jit(cholesky)/cholesky | solution.py:50
  525.6 9.8 %custom-call.31 = f32[1,128,128]{1,2,0:T(8,128)S(1)} custom-call(f32[1,128,128]{2,1,0:T(8,128)S(1)} %get-tuple-element.86), custom_call_target="InvertDiagBlocksLowerTriangular" | custom-call | tf_op jit(solution)/shard_map/jit(cholesky)/cholesky | solution.py:50
  538.0 11.7 %cholesky.377 = f32[128,128]{1,0:T(8,128)S(1)} custom-call(f32[128,128]{1,0:T(8,128)S(1)} %cholesky.443), custom_call_target="Cholesky" | custom-call | tf_op jit(solution)/shard_map/jit(cholesky)/cholesky | solution.py:50
  551.1 10.2 %custom-call.32 = f32[1,128,128]{1,2,0:T(8,128)S(1)} custom-call(f32[1,128,128]{2,1,0:T(8,128)S(1)} %get-tuple-element.83), custom_call_target="InvertDiagBlocksLowerTriangular" | custom-call | tf_op jit(solution)/shard_map/jit(cholesky)/cholesky | solution.py:50
  562.8 11.7 %cholesky.398 = f32[128,128]{1,0:T(8,128)S(1)} custom-call(f32[128,128]{1,0:T(8,128)S(1)} %cholesky.448), custom_call_target="Cholesky" | custom-call | tf_op jit(solution)/shard_map/jit(cholesky)/cholesky | solution.py:50
  575.3 9.8 %custom-call.33 = f32[1,128,128]{1,2,0:T(8,128)S(1)} custom-call(f32[1,128,128]{2,1,0:T(8,128)S(1)} %get-tuple-element.80), custom_call_target="InvertDiagBlocksLowerTriangular" | custom-call | tf_op jit(solution)/shard_map/jit(cholesky)/cholesky | solution.py:50
  586.5 11.8 %cholesky.415 = f32[128,128]{1,0:T(8,128)S(1)} custom-call(f32[128,128]{1,0:T(8,128)S(1)} %convolution_subtract_fusion.10), custom_call_target="Cholesky" | custom-call | tf_op jit(solution)/shard_map/jit(cholesky)/cholesky | solution.py:50
  602.7 11.7 %while.7 = (s32[]{:T(128)}, f32[512,512]{1,0:T(8,128)}, s32[4,2]{0,1:T(2,128)S(1)}, f32[4,128,128]{2,1,0:T(8,128)S(1)}, s32[]{:T(128)}) while((s32[]{:T(128)}, f32[512,512]{1,0:T(8,128)}, s32[4,2]{0,1:T(2,128)S(1)}, f32[4,128,128]{2,1,0:T(8,128)S(1)}, s32[]{:T(128)}) %tuple.82), condition=%wide.while_cond.2.clone, body=%wide.while_body.2.clone.sunk | while | flops 2 | bytes 131181 | solution.py:51
  603.4 2.3 bitcast_dynamic-update-slice_fusion.5
  606.3 2.3 bitcast_dynamic-update-slice_fusion.5
  609.2 2.3 bitcast_dynamic-update-slice_fusion.5
  612.2 2.2 bitcast_dynamic-update-slice_fusion.5
  614.4 39.3 %custom-call.34 = f32[4,128,128]{1,2,0:T(8,128)S(1)} custom-call(f32[4,128,128]{2,1,0:T(8,128)S(1)} %get-tuple-element.46), custom_call_target="InvertDiagBlocksLowerTriangular" | custom-call | tf_op jit(solution)/shard_map/jit(_solve_triangular)/triangular_solve | solution.py:51
  655.8 1.3 convolution_subtract_fusion
  657.5 1.6 convolution_subtract_fusion.4
  659.9 1.8 copy.10
  (107 shorter events, 34.9 us)
Async XLA Ops:
  6.5 59.6 %all-reduce.10.cloned.1.call-start = ((), (), s32[]{:S(2)}) async-start(), calls=%async_computation | async-start | bytes 2097152 | tf_op jit(solution)/shard_map/psum | solution.py:12
  8.1 58.1 %copy-start = (f32[512,512]{1,0:T(8,128)S(1)}, f32[512,512]{1,0:T(8,128)}, u32[]{:S(2)}) copy-start(f32[512,512]{1,0:T(8,128)} %param.10) | copy-start | bytes 3145732
  9.8 113.9 %all-reduce.12.cloned.1.call-start = ((), (), s32[]{:S(2)}) async-start(), calls=%async_computation.1 | async-start | bytes 2097152 | tf_op jit(solution)/shard_map/psum | solution.py:47
  71.9 110.4 %all-reduce.14.cloned.1.call-start = ((), (), s32[]{:S(2)}) async-start(), calls=%async_computation.2 | async-start | bytes 2097152 | tf_op jit(solution)/shard_map/psum | solution.py:12
  126.5 266.8 %all-reduce.20.cloned.1.call-start = ((), (), s32[]{:S(2)}) async-start(), calls=%async_computation.5 | async-start | bytes 4194304 | tf_op jit(solution)/shard_map/psum | solution.py:12
  182.4 1.7 copy-start.1
  184.3 1.0 copy-start.7
  233.1 90.9 %copy-start.3 = (f32[512,512]{1,0:T(8,128)S(1)}, f32[512,512]{1,0:T(8,128)}, u32[]{:S(2)}) copy-start(f32[512,512]{1,0:T(8,128)} %get-tuple-element.72) | copy-start | bytes 3145732
  331.8 120.5 %all-reduce.16.cloned.1.call-start = ((), (), s32[]{:S(2)}) async-start(), calls=%async_computation.3 | async-start | bytes 2097152 | tf_op jit(solution)/shard_map/psum | solution.py:47
  393.3 4.8 copy-start.8
  398.1 3.2 copy-start.5
  401.0 109.8 %all-reduce.18.cloned.1.call-start = ((), (), s32[]{:S(2)}) async-start(), calls=%async_computation.4 | async-start | bytes 2097152 | tf_op jit(solution)/shard_map/psum | solution.py:12
  510.9 1.7 copy-start.2
  512.8 1.0 copy-start.6
  562.8 90.9 %copy-start.4 = (f32[512,512]{1,0:T(8,128)S(1)}, f32[512,512]{1,0:T(8,128)}, u32[]{:S(2)}) copy-start(f32[512,512]{1,0:T(8,128)} %get-tuple-element.70) | copy-start | bytes 3145732
Sparse Core Ops, SparseCore 0:
  10.5 55.6 all-reduce.9
  72.1 51.5 all-reduce.11
  126.8 55.5 all-reduce.13
  331.9 61.3 all-reduce.19
  401.2 51.0 all-reduce.15
  455.3 55.5 all-reduce.17
where the time goes:
time: 678 us; the launch traced here: 669 us
  waiting for transfers between devices  328 us (48%)
  other arithmetic  250 us (37%)
  matrix products  35.9 us (5%)
  local copies, waits for them, and re-layouts  34.9 us (5%)
  between operations  19.2 us (3%)
    psum x4, waiting for transfers between devices, spread(): return lax.psum(jnp.where(mine, array, jnp.zeros_like(array)), axis)  228 us
    another operation x29, other arithmetic, body(): diag_factor = jnp.linalg.cholesky(block)  158 us
    psum x2, waiting for transfers between devices, body(): summed = lax.psum(partial_value, 'depth')  99.3 us
    another operation x5, other arithmetic, body(): jax.scipy.linalg.solve_triangular(diag_factor, update.T, lower=True)  81 us
    another operation x27, local copies, waits for them, and re-layouts, body(): jax.scipy.linalg.solve_triangular(diag_factor, update.T, lower=True)  22.6 us
  transfers between devices with their start and end apart: 6, of which 6 were waited for; matrix products, arithmetic and copies ran while one was open for 1% of the time, Pallas kernels for 0%

commit v1 on v0

v1 whole, which is shorter than its diff:
```python
import functools

import jax
import jax.numpy as jnp
from jax import lax
from jax.experimental import pallas as pl
from jax.experimental.pallas import tpu as pltpu
from jax.sharding import PartitionSpec as P

MESH = pl.DeviceIdType.MESH
F32 = jnp.float32
BF16 = jnp.bfloat16
BLK = 256
SUB = 128
VMEM_LIMIT = 60 * 1024 * 1024
LOW, HIGH = 2.0, 12.0


def ring_next(r, n, flip):
    if n == 4:
        y, x = r // 2, r % 2
        return (1 - x) * 2 + y if flip else x * 2 + (1 - y)
    return lax.rem(r + n - 1, n) if flip else lax.rem(r + 1, n)


def at(row, col, depth):
    return {"row": row, "col": col, "depth": depth}


def greet(nrow, ncol, ndepth):
    row, col, dep = lax.axis_index("row"), lax.axis_index("col"), lax.axis_index("depth")
    barrier = pltpu.get_barrier_semaphore()
    count = 0
    for s in range(1, ndepth):
        pl.semaphore_signal(barrier, inc=1, device_id=at(row, col, lax.rem(dep + s, ndepth)), device_id_type=MESH)
        count += 1
    for s in range(1, ncol):
        pl.semaphore_signal(barrier, inc=1, device_id=at(row, lax.rem(col + s, ncol), dep), device_id_type=MESH)
        count += 1
    for s in range(1, nrow):
        pl.semaphore_signal(barrier, inc=1, device_id=at(lax.rem(row + s, nrow), col, dep), device_id_type=MESH)
        count += 1
    pl.semaphore_wait(barrier, count)


def gather_kernel(nrow, ncol, ndepth, chunks, own, top, ring_send, ring_recv, side_send, side_recv0, side_recv1):
    greet(nrow, ncol, ndepth)
    spread_all(nrow, ncol, own, top, (own.shape[1],) * 2, chunks, (ring_send, ring_recv, side_send, (side_recv0, side_recv1)))


def spread_all(nrow, ncol, own, top, widths, chunks, sems, ready=None):
    row, col, dep = lax.axis_index("row"), lax.axis_index("col"), lax.axis_index("depth")
    ring_send, ring_recv, side_send, side_recv = sems
    size = own.shape[0] // chunks

    def part(ref, k, half, width):
        return ref.at[pl.ds(k * size, size), pl.ds(half * (width // 2), width // 2)]

    for owner in range(2):
        width = widths[owner]
        held = top.at[owner]

        def hop(k, half, src):
            return pltpu.make_async_remote_copy(
                src_ref=part(src, k, half, width), dst_ref=part(held, k, half, width),
                send_sem=ring_send.at[half, k], recv_sem=ring_recv.at[half, k],
                device_id=at(ring_next(row, nrow, half == 1), col, dep), device_id_type=MESH)

        def side(s, k, half, src):
            return pltpu.make_async_remote_copy(
                src_ref=part(src, k, half, width), dst_ref=part(held, k, half, width),
                send_sem=side_send.at[s - 1, half, k], recv_sem=side_recv[owner].at[half, k],
                device_id=at(row, lax.rem(col + s, ncol), dep), device_id_type=MESH)

        def goes_on(half):
            return ring_next(row, nrow, half == 1) != 0

        @pl.when(jnp.logical_and(col == owner, row == 0))
        def _():
            for k in range(chunks):
                if ready is not None:
                    ready(k)
                for half in range(2):
                    hop(k, half, own).start()
                    for s in range(1, ncol):
                        side(s, k, half, own).start()
            for k in range(chunks):
                for half in range(2):
                    hop(k, half, own).wait_send()
                    for s in range(1, ncol):
                        side(s, k, half, own).wait_send()
            held[:, pl.ds(0, width)] = own[:, pl.ds(0, width)]

        @pl.when(jnp.logical_and(col == owner, row != 0))
        def _():
            for k in range(chunks):
                for half in range(2):
                    hop(k, half, held).wait_recv()

                    @pl.when(goes_on(half))
                    def _():
                        hop(k, half, held).start()
                    for s in range(1, ncol):
                        side(s, k, half, held).start()
            for k in range(chunks):
                for half in range(2):
                    @pl.when(goes_on(half))
                    def _():
                        hop(k, half, held).wait_send()
                    for s in range(1, ncol):
                        side(s, k, half, held).wait_send()

        @pl.when(col != owner)
        def _():
            for k in range(chunks):
                for half in range(2):
                    side(1, k, half, held).wait_recv()


def reduce_kernel(nrow, ncol, ndepth, widths, part_ref, a_ref, own, top,
                  got, rs_send, rs_recv, ag_send, ag_recv, ring_send, ring_recv, side_send, side_recv0, side_recv1):
    row, col, dep = lax.axis_index("row"), lax.axis_index("col"), lax.axis_index("depth")
    size = own.shape[0] // ndepth
    greet(nrow, ncol, ndepth)

    def rows(index):
        return pl.ds(pl.multiple_of(index * size, size), size)

    def scatter(s):
        other = lax.rem(dep + s, ndepth)
        return pltpu.make_async_remote_copy(
            src_ref=part_ref.at[rows(other)], dst_ref=got.at[s - 1],
            send_sem=rs_send.at[s - 1], recv_sem=rs_recv.at[s - 1],
            device_id=at(row, col, other), device_id_type=MESH)

    def share(s):
        return pltpu.make_async_remote_copy(
            src_ref=own.at[rows(dep)], dst_ref=own.at[rows(dep)],
            send_sem=ag_send.at[s - 1], recv_sem=ag_recv.at[s - 1],
            device_id=at(row, col, lax.rem(dep + s, ndepth)), device_id_type=MESH)

    for s in range(1, ndepth):
        scatter(s).start()
    total = part_ref[rows(dep), :]
    for s in range(1, ndepth):
        scatter(s).wait_recv()
        total = total + got[s - 1]
    own[rows(dep), :] = a_ref[rows(dep), :] - total
    for s in range(1, ndepth):
        share(s).start()
    for s in range(1, ndepth):
        other = lax.rem(dep + ndepth - s, ndepth)
        pltpu.make_async_remote_copy(
            src_ref=own.at[rows(other)], dst_ref=own.at[rows(other)],
            send_sem=ag_send.at[s - 1], recv_sem=ag_recv.at[s - 1],
            device_id=at(row, col, other), device_id_type=MESH).wait_recv()
    for s in range(1, ndepth):
        scatter(s).wait_send()
        share(s).wait_send()
    spread_all(nrow, ncol, own, top, widths, ndepth, (ring_send, ring_recv, side_send, (side_recv0, side_recv1)))


def split(x):
    high = x.astype(BF16)
    return high, (x - high.astype(F32)).astype(BF16)


NN = (((1,), (0,)), ((), ()))
NT = (((1,), (1,)), ((), ()))
TN = (((0,), (0,)), ((), ()))


def dot1(x, y, dims):
    return lax.dot_general(x, y, dims, preferred_element_type=F32)


def dot3(x, y, dims):
    (xh, xl), (yh, yl) = x, y
    return dot1(xh, yh, dims) + (dot1(xh, yl, dims) + dot1(xl, yh, dims))


def eye(n):
    return (lax.broadcasted_iota(jnp.int32, (n, n), 0) == lax.broadcasted_iota(jnp.int32, (n, n), 1)).astype(F32)


def inverses(blocks):
    unit = eye(blocks[0].shape[0])
    mid, rad = (HIGH + LOW) / 2, (HIGH - LOW) / 2
    t2 = 2 * (mid / rad) ** 2 - 1
    c1, c2 = 4 * mid / (rad * rad * t2), -2 / (rad * rad * t2)
    xs = [c1 * unit + c2 * b for b in blocks]
    halves = [split(b) for b in blocks]
    for step in range(5):
        if step < 2:
            xs = [x.astype(BF16).astype(F32) for x in xs]
            es = [unit - dot1(h[0], x.astype(BF16), NN) for h, x in zip(halves, xs)]
            xs = [x + dot1(x.astype(BF16), e.astype(BF16), NN) for x, e in zip(xs, es)]
        else:
            ss = [split(x) for x in xs]
            es = [unit - dot3(h, s, NN) for h, s in zip(halves, ss)]
            xs = [x + dot1(s[0], e.astype(BF16), NN) if step == 4 else x + dot3(s, split(e), NN)
                  for x, s, e in zip(xs, ss, es)]
    return xs


def base_cholesky(mats, n, count):
    sub = lax.broadcasted_iota(jnp.int32, (count, 8, n), 1)
    lane = lax.broadcasted_iota(jnp.int32, (count, 8, n), 2)
    for j in range(n // 8):
        r = mats[:, 8 * j:8 * j + 8, :]
        for t in range(8):
            c = 8 * j + t
            column = r[:, :, c:c + 1]
            d = column[:, t:t + 1, :]
            inv = lax.rsqrt(d)
            inv = inv * (1.5 - 0.5 * d * inv * inv)
            u = r[:, t:t + 1, :] * inv
            r = jnp.where(sub > t, r - (column * inv) * u, jnp.where(sub == t, u, r))
        r = jnp.where(lane >= sub + 8 * j, r, 0.0)
        mats[:, 8 * j:8 * j + 8, :] = r
        if j + 1 < n // 8:
            high = r.astype(BF16).astype(F32)
            low = r - high
            left = jnp.concatenate([high, high, low], axis=1).astype(BF16)
            right = jnp.concatenate([high, low, high], axis=1).astype(BF16)
            start = 8 * (j + 1)
            for b in range(count):
                out = dot1(left[b], right[b], TN)
                mats[b, start:, :] = mats[b, start:, :] - out[start:, :]


def factor_kernel(own_ref, top_ref, out_ref, work, mh, ml, uh, ul, mats, inner):
    nb, width = top_ref.shape[1], own_ref.shape[1]
    rows = own_ref.shape[0]
    for half in range(2):
        work[half * nb:(half + 1) * nb, :(half + 1) * nb] = top_ref[half, :, :(half + 1) * nb]
    work[width:width + rows, :] = own_ref[...]
    steps = width // BLK
    for k in range(steps):
        lo, hi = k * BLK, (k + 1) * BLK
        if k > 0:
            right = (uh[lo:hi, :lo], ul[lo:hi, :lo])
            for r in range(lo, width + rows, BLK):
                left = (mh[r:r + BLK, :lo], ml[r:r + BLK, :lo])
                work[r:r + BLK, lo:hi] = work[r:r + BLK, lo:hi] - dot3(left, right, NT)
        inv = split(inverses([work[lo:hi, lo:hi]])[0])
        for r in range(hi, width + rows, BLK):
            u = split(work[r:r + BLK, lo:hi])
            uh[r:r + BLK, lo:hi], ul[r:r + BLK, lo:hi] = u
            m = dot3(u, inv, NN)
            mh[r:r + BLK, lo:hi], ml[r:r + BLK, lo:hi] = split(m)
    diag = [work[k * BLK:(k + 1) * BLK, k * BLK:(k + 1) * BLK] for k in range(steps)]
    invs = inverses([d[:SUB, :SUB] for d in diag])
    for k in range(steps):
        lo, mid, hi = k * BLK, k * BLK + SUB, (k + 1) * BLK
        low = split(work[mid:hi, lo:mid])
        m = split(dot3(low, split(invs[k]), NN))
        inner[k] = m[0].astype(F32) + m[1].astype(F32)
        mats[2 * k] = work[lo:mid, lo:mid]
        mats[2 * k + 1] = work[mid:hi, mid:hi] - dot3(m, low, NT)
    base_cholesky(mats, SUB, 2 * steps)
    position = lax.axis_index("row") * lax.axis_size("col") + lax.axis_index("col")
    first = position * rows
    for k in range(steps):
        lo, mid, hi = k * BLK, k * BLK + SUB, (k + 1) * BLK
        t1, t2 = split(mats[2 * k]), split(mats[2 * k + 1])
        l21 = split(dot3(split(inner[k]), t1, NT))
        for r in range(0, rows, BLK):
            w = width + r
            p1 = (mh[w:w + BLK, lo:mid], ml[w:w + BLK, lo:mid])
            p2 = (mh[w:w + BLK, mid:hi], ml[w:w + BLK, mid:hi])
            x1 = dot3(p1, t1, NT) + dot3(p2, l21, NN)
            x2 = dot3(p2, t2, NT)
            ids = first + r + lax.broadcasted_iota(jnp.int32, (BLK, SUB), 0)
            cols = lax.broadcasted_iota(jnp.int32, (BLK, SUB), 1)
            out_ref[r:r + BLK, lo:mid] = jnp.where(ids >= lo + cols, x1, 0.0)
            out_ref[r:r + BLK, mid:hi] = jnp.where(ids >= mid + cols, x2, 0.0)


def vmem(n):
    return [pl.BlockSpec(memory_space=pltpu.VMEM)] * n


def spread_sems(ncol, chunks):
    dma = pltpu.SemaphoreType.DMA
    return [dma((2, chunks)), dma((2, chunks)), dma((ncol - 1, 2, chunks)), dma((2, chunks)), dma((2, chunks))]


def solution(mesh):
    nrow, ncol, ndepth = (mesh.shape[name] for name in ("row", "col", "depth"))
    chunks = 4

    def body(a_cols, past_panels):
        rows, width = a_cols.shape
        past = past_panels.shape[1]
        top = pl.pallas_call(
            functools.partial(gather_kernel, nrow, ncol, ndepth, chunks),
            out_shape=jax.ShapeDtypeStruct((2, rows, past), F32),
            in_specs=vmem(1), out_specs=vmem(1)[0],
            scratch_shapes=spread_sems(ncol, chunks),
            compiler_params=pltpu.CompilerParams(collective_id=0, has_side_effects=True),
        )(past_panels)
        partial = lax.dot_general(past_panels, top.reshape(2 * rows, past), NT,
                                  precision=lax.Precision.HIGH, preferred_element_type=F32)
        dma = pltpu.SemaphoreType.DMA
        own, head = pl.pallas_call(
            functools.partial(reduce_kernel, nrow, ncol, ndepth, (rows, 2 * rows)),
            out_shape=[jax.ShapeDtypeStruct((rows, width), F32), jax.ShapeDtypeStruct((2, rows, width), F32)],
            in_specs=vmem(2), out_specs=vmem(2),
            scratch_shapes=[pltpu.VMEM((ndepth - 1, rows // ndepth, width), F32)]
            + [dma((ndepth - 1,))] * 4 + spread_sems(ncol, ndepth),
            compiler_params=pltpu.CompilerParams(collective_id=1, has_side_effects=True, vmem_limit_bytes=VMEM_LIMIT),
        )(partial, a_cols)
        halves = [pltpu.VMEM((width + rows, width), BF16)] * 4
        return pl.pallas_call(
            factor_kernel,
            out_shape=jax.ShapeDtypeStruct((rows, width), F32),
            in_specs=vmem(2), out_specs=vmem(1)[0],
            scratch_shapes=[pltpu.VMEM((width + rows, width), F32)] + halves
            + [pltpu.VMEM((width // SUB, SUB, SUB), F32), pltpu.VMEM((width // BLK, SUB, SUB), F32)],
            compiler_params=pltpu.CompilerParams(vmem_limit_bytes=VMEM_LIMIT),
        )(own, head)

    in_specs = (P(("row", "col"), None), P(("row", "col"), "depth"))
    out_specs = P(("row", "col"), None)
    return jax.shard_map(body, mesh=mesh, in_specs=in_specs, out_specs=out_specs, check_vma=False)
```

time: 678 us -> 407 us (0.60); the launches traced: 669 us -> 407 us
  Pallas kernels: 0 us -> 402 us
  waiting for transfers between devices: 328 us -> 0 us
  other arithmetic: 250 us -> 0 us
  local copies, waits for them, and re-layouts: 34.9 us -> 0.01 us
  matrix products: 35.9 us -> 4.75 us
  between operations: 19.2 us -> 0.03 us
    pallas_call x0 -> x3, Pallas kernels: none -> 402 us  [the longest x1 240 us: body(): pl.pallas_call(functools.partial(reduce_kernel, nrow, ncol, ndepth, (rows...]
    psum x6 -> x0, waiting for transfers between devices: 328 us -> none  [the longest x4 228 us: spread(): return lax.psum(jnp.where(mine, array, jnp.zeros_like(array)), axis)]
    another operation x36 -> x0, other arithmetic: 241 us -> none  [the longest x29 158 us: body(): diag_factor = jnp.linalg.cholesky(block)]
    another operation x35 -> x0, local copies, waits for them, and re-layouts: 22.9 us -> none  [the longest x27 22.6 us: body(): jax.scipy.linalg.solve_triangular(diag_factor, update.T, lower=True)]
    another operation x26 -> x0, matrix products: 22.5 us -> none  [the longest x14 11.6 us: body(): jax.scipy.linalg.solve_triangular(diag_factor, update.T, lower=True)]
    dot_general x3 -> x1, matrix products: 13.4 us -> 4.75 us  [body(): lax.dot_general(past_panels, top.reshape(2 * rows, past), NT, precision=l...]
    select_n x5 -> x0, other arithmetic: 8.56 us -> none  [the longest x4 8.42 us: spread(): return lax.psum(jnp.where(mine, array, jnp.zeros_like(array)), axis)]
  transfers between devices with their start and end apart: 6 -> 0, of which waited for: 6 -> 0; matrix products, arithmetic and copies ran while one was open for 1% -> 0% of each run, Pallas kernels for 0% -> 0%
where the time goes in v1:
time: 407 us
  Pallas kernels  402 us (99%)
  matrix products  4.75 us (1%)
    pallas_call x1, Pallas kernels, body(): pl.pallas_call(functools.partial(reduce_kernel, nrow, ncol, ndepth, (rows...  240 us
    pallas_call x1, Pallas kernels, body(): pl.pallas_call(functools.partial(gather_kernel, nrow, ncol, ndepth, chunk...  124 us
    pallas_call x1, Pallas kernels, body(): pl.pallas_call(factor_kernel, out_shape=jax.ShapeDtypeStruct((rows, width...  38 us

profile of v1, /device:TPU:27, one launch (start us, length us, event | category | flops | bytes accessed | tf_op | source)
XLA Modules:
  0.0 406.7 jit_solution(16528512467311819097)
XLA Ops:
  0.0 0.0 copy-start
  0.0 124.1 %shard_map.28 = f32[2,512,512]{2,1,0:T(8,128)} custom-call(f32[512,512]{1,0:T(8,128)} %own.1), custom_call_target="tpu_custom_call" | custom-call | tf_op jit(solution)/shard_map/pallas_call | solution.py:296
  124.1 0.0 copy-done
  124.1 4.8 %fusion.part_ref = f32[512,1024]{1,0:T(8,128)} fusion(f32[512,512]{1,0:T(8,128)S(1)} %copy-done, f32[1024,512]{1,0:T(8,128)} %bitcast.3), kind=kOutput, calls=%fused_computation | convolution fusion | flops 1610612736 | bytes 5242880 | tf_op jit(solution)/shard_map/dot_general | solution.py:303
  128.9 239.9 %shard_map.29 = (f32[512,1024]{1,0:T(8,128)}, f32[2,512,1024]{2,1,0:T(8,128)}) custom-call(f32[512,1024]{1,0:T(8,128)} %fusion.part_ref, f32[512,1024]{1,0:T(8,128)} %a_ref.1), custom_call_target="tpu_custom_call" | custom-call | tf_op jit(solution)/shard_map/pallas_call | solution.py:306
  368.7 38.0 %shard_map.30 = f32[512,1024]{1,0:T(8,128)} custom-call(f32[512,1024]{1,0:T(8,128)} %get-tuple-element.7.own_ref, f32[2,512,1024]{2,1,0:T(8,128)} %get-tuple-element.8.top_ref), custom_call_target="tpu_custom_call" | custom-call | tf_op jit(solution)/shard_map/pallas_call | solution.py:315
Async XLA Ops:
  0.0 124.1 %copy-start = (f32[512,512]{1,0:T(8,128)S(1)}, f32[512,512]{1,0:T(8,128)}, u32[]{:S(2)}) copy-start(f32[512,512]{1,0:T(8,128)} %own.1) | copy-start | bytes 3145732

commit v2 on v1

--- a/solution.py
+++ b/solution.py
@@ -17,10 +17,14 @@
 
 
 def ring_next(r, n, flip):
+    return tour(r, n, flip)
+
+
+def tour(r, n, flip):
     if n == 4:
         y, x = r // 2, r % 2
         return (1 - x) * 2 + y if flip else x * 2 + (1 - y)
-    return lax.rem(r + n - 1, n) if flip else lax.rem(r + 1, n)
+    return (r + n - 1) % n if flip else (r + 1) % n
 
 
 def at(row, col, depth):
@@ -43,82 +47,81 @@
     pl.semaphore_wait(barrier, count)
 
 
-def gather_kernel(nrow, ncol, ndepth, chunks, own, top, ring_send, ring_recv, side_send, side_recv0, side_recv1):
+def gather_kernel(nrow, ncol, ndepth, chunks, own, top, *sems):
     greet(nrow, ncol, ndepth)
-    spread_all(nrow, ncol, own, top, (own.shape[1],) * 2, chunks, (ring_send, ring_recv, side_send, (side_recv0, side_recv1)))
-
-
-def spread_all(nrow, ncol, own, top, widths, chunks, sems, ready=None):
+    order = list(range(chunks))
+    spread(nrow, ncol, own, top, (own.shape[1],) * 2, own.shape[0] // chunks, order, sems)
+
+
+def arrivals(r, n, chunks):
+    tours = []
+    for half in range(2):
+        place, hops = 0, 0
+        while place != r:
+            place, hops = int(tour(place, n, half == 1)), hops + 1
+        tours.append(hops)
+    events = [(k + tours[half], half, k) for k in range(chunks) for half in range(2)]
+    return [(k, half) for _, half, k in sorted(events)]
+
+
+def spread(nrow, ncol, own, top, widths, size, order, sems, ready=None):
     row, col, dep = lax.axis_index("row"), lax.axis_index("col"), lax.axis_index("depth")
-    ring_send, ring_recv, side_send, side_recv = sems
-    size = own.shape[0] // chunks
+    ring_send, ring_recv, side_send, *side_recv = sems
+    chunks = len(order)
 
     def part(ref, k, half, width):
-        return ref.at[pl.ds(k * size, size), pl.ds(half * (width // 2), width // 2)]
+        slab = order[k] * size if isinstance(order[k], int) else pl.multiple_of(order[k] * size, size)
+        return ref.at[pl.ds(slab, size), pl.ds(half * (width // 2), width // 2)]
+
+    def hop(owner, k, half, src):
+        return pltpu.make_async_remote_copy(
+            src_ref=part(src, k, half, widths[owner]), dst_ref=part(top.at[owner], k, half, widths[owner]),
+            send_sem=ring_send.at[half, k], recv_sem=ring_recv.at[half, k],
+            device_id=at(ring_next(row, nrow, half == 1), col, dep), device_id_type=MESH)
+
+    def side(owner, s, k, half, src):
+        return pltpu.make_async_remote_copy(
+            src_ref=part(src, k, half, widths[owner]), dst_ref=part(top.at[owner], k, half, widths[owner]),
+            send_sem=side_send.at[s - 1, half, k], recv_sem=side_recv[owner].at[half, k],
+            device_id=at(row, lax.rem(col + s, ncol), dep), device_id_type=MESH)
 
     for owner in range(2):
-        width = widths[owner]
         held = top.at[owner]
-
-        def hop(k, half, src):
-            return pltpu.make_async_remote_copy(
-                src_ref=part(src, k, half, width), dst_ref=part(held, k, half, width),
-                send_sem=ring_send.at[half, k], recv_sem=ring_recv.at[half, k],
-                device_id=at(ring_next(row, nrow, half == 1), col, dep), device_id_type=MESH)
-
-        def side(s, k, half, src):
-            return pltpu.make_async_remote_copy(
-                src_ref=part(src, k, half, width), dst_ref=part(held, k, half, width),
-                send_sem=side_send.at[s - 1, half, k], recv_sem=side_recv[owner].at[half, k],
-                device_id=at(row, lax.rem(col + s, ncol), dep), device_id_type=MESH)
-
-        def goes_on(half):
-            return ring_next(row, nrow, half == 1) != 0
-
-        @pl.when(jnp.logical_and(col == owner, row == 0))
-        def _():
-            for k in range(chunks):
-                if ready is not None:
-                    ready(k)
-                for half in range(2):
-                    hop(k, half, own).start()
+        for r in range(nrow):
+            src = own if r == 0 else held
+
+            @pl.when(jnp.logical_and(col == owner, row == r))
+            def _():
+                seen = -1
+                events = [(k, half) for k in range(chunks) for half in range(2)] if r == 0 else arrivals(r, nrow, chunks)
+                last = [r != 0 and int(tour(r, nrow, half == 1)) == 0 for half in range(2)]
+                for k, half in events:
+                    if r != 0:
+                        hop(owner, k, half, held).wait_recv()
+                    elif ready is not None and k > seen:
+                        ready(k)
+                        seen = k
+                    if not last[half]:
+                        hop(owner, k, half, src).start()
                     for s in range(1, ncol):
-                        side(s, k, half, own).start()
-            for k in range(chunks):
-                for half in range(2):
-                    hop(k, half, own).wait_send()
+                        side(owner, s, k, half, src).start()
+                if r == 0:
+                    held[:, pl.ds(0, widths[owner])] = own[:, pl.ds(0, widths[owner])]
+                for k, half in events:
+                    if not last[half]:
+                        hop(owner, k, half, src).wait_send()
                     for s in range(1, ncol):
-                        side(s, k, half, own).wait_send()
-            held[:, pl.ds(0, width)] = own[:, pl.ds(0, width)]
-
-        @pl.when(jnp.logical_and(col == owner, row != 0))
-        def _():
-            for k in range(chunks):
-                for half in range(2):
-                    hop(k, half, held).wait_recv()
-
-                    @pl.when(goes_on(half))
-                    def _():
-                        hop(k, half, held).start()
-                    for s in range(1, ncol):
-                        side(s, k, half, held).start()
-            for k in range(chunks):
-                for half in range(2):
-                    @pl.when(goes_on(half))
-                    def _():
-                        hop(k, half, held).wait_send()
-                    for s in range(1, ncol):
-                        side(s, k, half, held).wait_send()
-
+                        side(owner, s, k, half, src).wait_send()
+
+    for owner in range(2):
         @pl.when(col != owner)
         def _():
             for k in range(chunks):
                 for half in range(2):
-                    side(1, k, half, held).wait_recv()
-
-
-def reduce_kernel(nrow, ncol, ndepth, widths, part_ref, a_ref, own, top,
-                  got, rs_send, rs_recv, ag_send, ag_recv, ring_send, ring_recv, side_send, side_recv0, side_recv1):
+                    side(owner, 1, k, half, top.at[owner]).wait_recv()
+
+
+def reduce_kernel(nrow, ncol, ndepth, widths, part_ref, a_ref, own, top, got, rs_send, rs_recv, ag_send, ag_recv, *sems):
     row, col, dep = lax.axis_index("row"), lax.axis_index("col"), lax.axis_index("depth")
     size = own.shape[0] // ndepth
     greet(nrow, ncol, ndepth)
@@ -139,25 +142,32 @@
             send_sem=ag_send.at[s - 1], recv_sem=ag_recv.at[s - 1],
             device_id=at(row, col, lax.rem(dep + s, ndepth)), device_id_type=MESH)
 
-    for s in range(1, ndepth):
-        scatter(s).start()
-    total = part_ref[rows(dep), :]
-    for s in range(1, ndepth):
-        scatter(s).wait_recv()
-        total = total + got[s - 1]
-    own[rows(dep), :] = a_ref[rows(dep), :] - total
-    for s in range(1, ndepth):
-        share(s).start()
-    for s in range(1, ndepth):
+    def arrived(s):
         other = lax.rem(dep + ndepth - s, ndepth)
         pltpu.make_async_remote_copy(
             src_ref=own.at[rows(other)], dst_ref=own.at[rows(other)],
             send_sem=ag_send.at[s - 1], recv_sem=ag_recv.at[s - 1],
             device_id=at(row, col, other), device_id_type=MESH).wait_recv()
+
+    for s in range(1, ndepth):
+        scatter(s).start()
+    total = part_ref[rows(dep), :]
+    for s in range(1, ndepth):
+        scatter(s).wait_recv()
+        total = total + got[s - 1]
+    own[rows(dep), :] = a_ref[rows(dep), :] - total
+    for s in range(1, ndepth):
+        share(s).start()
+    order = [lax.rem(dep + ndepth - s, ndepth) for s in range(ndepth)]
+    spread(nrow, ncol, own, top, widths, size, order, sems, ready=lambda s: arrived(s) if s else None)
+
+    @pl.when(jnp.logical_or(row != 0, col >= 2))
+    def _():
+        for s in range(1, ndepth):
+            arrived(s)
     for s in range(1, ndepth):
         scatter(s).wait_send()
         share(s).wait_send()
-    spread_all(nrow, ncol, own, top, widths, ndepth, (ring_send, ring_recv, side_send, (side_recv0, side_recv1)))
 
 
 def split(x):

time: 407 us -> 197 us (0.48)
  Pallas kernels: 402 us -> 192 us
    pallas_call x1, Pallas kernels: 240 us -> 121 us  [body(): pl.pallas_call(functools.partial(reduce_kernel, nrow, ncol, ndepth, (rows...]
    pallas_call x1, Pallas kernels: 124 us -> 32.6 us  [body(): pl.pallas_call(functools.partial(gather_kernel, nrow, ncol, ndepth, chunk...]
where the time goes in v2:
time: 197 us
  Pallas kernels  192 us (97%)
  matrix products  4.75 us (2%)
    pallas_call x1, Pallas kernels, body(): pl.pallas_call(functools.partial(reduce_kernel, nrow, ncol, ndepth, (rows...  121 us
    pallas_call x1, Pallas kernels, body(): pl.pallas_call(factor_kernel, out_shape=jax.ShapeDtypeStruct((rows, width...  38.1 us
    pallas_call x1, Pallas kernels, body(): pl.pallas_call(functools.partial(gather_kernel, nrow, ncol, ndepth, chunk...  32.6 us
    dot_general x1, matrix products, body(): lax.dot_general(past_panels, top.reshape(2 * rows, past), NT, precision=l...  4.75 us

profile of v2, /device:TPU:27, one launch (start us, length us, event | category | flops | bytes accessed | tf_op | source)
XLA Modules:
  0.0 196.8 jit_solution(13114594659015457812)
XLA Ops:
  0.0 0.0 copy-start
  0.0 32.6 %shard_map.28 = f32[2,512,512]{2,1,0:T(8,128)} custom-call(f32[512,512]{1,0:T(8,128)} %own.1), custom_call_target="tpu_custom_call" | custom-call | tf_op jit(solution)/shard_map/pallas_call | solution.py:306
  32.7 0.0 copy-done
  32.7 4.8 %fusion.part_ref = f32[512,1024]{1,0:T(8,128)} fusion(f32[512,512]{1,0:T(8,128)S(1)} %copy-done, f32[1024,512]{1,0:T(8,128)} %bitcast.3), kind=kOutput, calls=%fused_computation | convolution fusion | flops 1610612736 | bytes 5242880 | tf_op jit(solution)/shard_map/dot_general | solution.py:313
  37.4 121.3 %shard_map.29 = (f32[512,1024]{1,0:T(8,128)}, f32[2,512,1024]{2,1,0:T(8,128)}) custom-call(f32[512,1024]{1,0:T(8,128)} %fusion.part_ref, f32[512,1024]{1,0:T(8,128)} %a_ref.1), custom_call_target="tpu_custom_call" | custom-call | tf_op jit(solution)/shard_map/pallas_call | solution.py:316
  158.8 38.1 %shard_map.30 = f32[512,1024]{1,0:T(8,128)} custom-call(f32[512,1024]{1,0:T(8,128)} %get-tuple-element.7.own_ref, f32[2,512,1024]{2,1,0:T(8,128)} %get-tuple-element.8.top_ref), custom_call_target="tpu_custom_call" | custom-call | tf_op jit(solution)/shard_map/pallas_call | solution.py:325
Async XLA Ops:
  0.0 32.7 %copy-start = (f32[512,512]{1,0:T(8,128)S(1)}, f32[512,512]{1,0:T(8,128)}, u32[]{:S(2)}) copy-start(f32[512,512]{1,0:T(8,128)} %own.1) | copy-start | bytes 3145732
